TPU v7x, 256 devices: a whole 4x4x8 slice. The times are simulated.
256 devices in a mesh: segment: 8 (over x, y_hi), dp: 32 (over y_lo, z, core).
Axes of the slice: x: 4, y: 4 (y_hi: 2, y_lo: 2; y = y_hi * 2 + y_lo), z: 8, core: 2. Of those that a mesh axis runs over, the one named last changes fastest.
Arguments:
- encoder_patch_input: bfloat16 [32, 1024, 1024], P('dp'), may hold values from -6 to 6
- encoder_norm_gains: float32 [8, 1024], P('segment'), may hold values from 0.5 to 1.5
- encoder_input_weight: bfloat16 [8, 1024, 2048], P('segment'), may hold values from -0.1875 to 0.1875
- encoder_output_weight: bfloat16 [8, 2048, 1024], P('segment'), may hold values from -0.125 to 0.125
- diffuser_hidden_states: bfloat16 [32, 1024, 2048], P('dp', 'segment'), may hold values from -6 to 6
- projector_first_weight: bfloat16 [2048, 2048], P('dp', 'segment'), may hold values from -0.125 to 0.125
- projector_second_weight: bfloat16 [2048, 1024], P(('segment', 'dp')), may hold values from -0.125 to 0.125
Outputs:
- grad_w1: float32 [2048, 2048], P('dp', 'segment')
- grad_w2: float32 [2048, 1024], P(('segment', 'dp'))
All inputs are finite; a program needn't handle non-finite values.
Results may differ from a plain program's by a relative error of at most 0.014.
Values may be sent and summed in bfloat16 or wider, within the bound.
A program may use at most 128 MiB of HBM per device.

v0:
```python
import jax
import jax.numpy as jnp
from jax import lax
from jax.sharding import PartitionSpec as P

norm_eps = 1e-06


def shifted(block, axis, distance):
    devices = range(lax.axis_size(axis))
    route = [(i - distance, i) for i in devices if i - distance in devices]
    return lax.ppermute(block, axis, route)


def from_root(block, axis, holder):
    block = jnp.where(lax.axis_index(axis) == holder, block, jnp.zeros_like(block))
    return lax.psum(block, axis)


def encoder_layer(hidden, scale_row, weight_in, weight_out):
    floats = hidden.astype(jnp.float32)
    normed = (
        floats * lax.rsqrt(jnp.mean(floats * floats, axis=-1, keepdims=True) + norm_eps) * scale_row
    )
    inner = jnp.dot(normed.astype(jnp.bfloat16), weight_in, preferred_element_type=jnp.float32)
    inner = jax.nn.gelu(inner, approximate=True).astype(jnp.bfloat16)
    return (floats + jnp.dot(inner, weight_out, preferred_element_type=jnp.float32)).astype(
        jnp.bfloat16
    )


def cosine_grad(projected, features):
    feat_f = features.astype(jnp.float32)
    squared = jnp.sum(projected * projected, axis=-1, keepdims=True) + norm_eps
    inv_proj = lax.rsqrt(squared)
    unit_feat = feat_f * lax.rsqrt(jnp.sum(feat_f * feat_f, axis=-1, keepdims=True) + norm_eps)
    cosine = jnp.sum(projected * unit_feat, axis=-1, keepdims=True) * inv_proj
    return (cosine * projected / squared - unit_feat * inv_proj).astype(jnp.bfloat16)


def silu_slope(preact):
    sigma = jax.nn.sigmoid(preact)
    return sigma * (1.0 + preact * (1.0 - sigma))


def contract_rows(left, right):
    return lax.dot_general(
        left, right, (((0,), (0,)), ((), ())), preferred_element_type=jnp.float32
    )


def on_device(
    encoder_patch_input,
    encoder_norm_gains,
    encoder_input_weight,
    encoder_output_weight,
    diffuser_hidden_states,
    projector_first_weight,
    projector_second_weight,
):
    segments = lax.axis_size("segment")
    segment_pos = lax.axis_index("segment")
    token_rows = diffuser_hidden_states.shape[1]
    source = encoder_patch_input[0]
    feat_width = source.shape[1]
    scale_row = encoder_norm_gains[0]
    weight_in = encoder_input_weight[0]
    weight_out = encoder_output_weight[0]

    def run_layer(entering):
        return encoder_layer(entering, scale_row, weight_in, weight_out)

    def pass_through(entering):
        return entering

    blank = jnp.zeros((token_rows, feat_width), jnp.bfloat16)
    inbound = blank
    finished = []
    for moment in range(2 * segments - 1):
        if moment < segments:
            inject = source[moment * token_rows : (moment + 1) * token_rows]
        else:
            inject = blank
        entering = jnp.where(segment_pos == 0, inject, inbound)
        active = jnp.logical_and(segment_pos <= moment, moment - segment_pos < segments)
        leaving = lax.cond(active, run_layer, pass_through, entering)
        if moment < 2 * segments - 2:
            inbound = shifted(leaving, "segment", 1)
        if moment >= segments - 1:
            finished.append(leaving)
    stacked = jnp.concatenate(finished, axis=0)
    everything = from_root(stacked, "segment", segments - 1)
    own_feats = lax.dynamic_slice_in_dim(everything, segment_pos * token_rows, token_rows, 0)
    first_block, second_block = (
        lax.all_gather(projector_first_weight, "dp", axis=0, tiled=True),
        lax.all_gather(projector_second_weight, "dp", axis=0, tiled=True),
    )
    hidden_combined = lax.all_gather(diffuser_hidden_states[0], "segment", axis=0, tiled=True)
    preact = jnp.dot(hidden_combined, first_block, preferred_element_type=jnp.float32)
    activated = jax.nn.silu(preact).astype(jnp.bfloat16)
    projected = lax.psum_scatter(
        jnp.dot(activated, second_block, preferred_element_type=jnp.float32),
        "segment",
        scatter_dimension=0,
        tiled=True,
    )
    grad_own = cosine_grad(projected, own_feats)
    grad_all = lax.all_gather(grad_own, "segment", axis=0, tiled=True)
    grad_second = contract_rows(activated, grad_all)
    back = lax.dot_general(
        grad_all, second_block, (((1,), (1,)), ((), ())), preferred_element_type=jnp.float32
    )
    grad_pre = (back * silu_slope(preact)).astype(jnp.bfloat16)
    grad_first = contract_rows(hidden_combined, grad_pre)
    first_rows, second_rows = (
        lax.psum_scatter(grad_first, "dp", scatter_dimension=0, tiled=True),
        lax.psum_scatter(grad_second, "dp", scatter_dimension=0, tiled=True),
    )
    return (first_rows, second_rows)


def solution(mesh):
    placed = (
        P("dp", None, None),
        P("segment", None),
        P("segment", None, None),
        P("segment", None, None),
        P("dp", "segment", None),
        P("dp", "segment"),
        P(("segment", "dp"), None),
    )
    return jax.shard_map(
        on_device,
        mesh=mesh,
        in_specs=placed,
        out_specs=(P("dp", "segment"), P(("segment", "dp"), None)),
        check_vma=False,
    )
```

profile of v0, /device:TPU:2, one launch (start us, length us, event | category | flops | bytes accessed | tf_op | source)
XLA Modules:
  0.0 760.4 jit_solution(12394751905636336380)
XLA Ops:
  9.0 5.2 collective-permute-start
  14.3 7.2 collective-permute-done
  21.5 4.2 collective-permute-start.1
  25.7 11.2 %collective-permute-done.1 = bf16[128,1024]{1,0:T(8,128)(2,1)S(1)} collective-permute-done((bf16[128,1024]{1,0:T(8,128)(2,1)S(1)}, bf16[128,1024]{1,0:T(8,128)(2,1)S(1)}, u32[]{:S(2)}, u32[]{:S(2)}) %collective-permute-start.1) | collective-permute-done | bytes 262176 | tf_op jit(solution)/shard_map/ppermute | solution.py:12
  36.9 5.3 conditional.17
  37.1 5.1 fusion.62
  44.2 8.8 %collective-permute-done.2 = bf16[128,1024]{1,0:T(8,128)(2,1)S(1)} collective-permute-done((bf16[128,1024]{1,0:T(8,128)(2,1)S(1)}, bf16[128,1024]{1,0:T(8,128)(2,1)S(1)}, u32[]{:S(2)}, u32[]{:S(2)}) %collective-permute-start.2) | collective-permute-done | bytes 262176 | tf_op jit(solution)/shard_map/ppermute | solution.py:12
  53.1 5.3 conditional.18
  53.3 5.1 fusion.93
  60.3 8.8 %collective-permute-done.3 = bf16[128,1024]{1,0:T(8,128)(2,1)S(1)} collective-permute-done((bf16[128,1024]{1,0:T(8,128)(2,1)S(1)}, bf16[128,1024]{1,0:T(8,128)(2,1)S(1)}, u32[]{:S(2)}, u32[]{:S(2)}) %collective-permute-start.3) | collective-permute-done | bytes 262176 | tf_op jit(solution)/shard_map/ppermute | solution.py:12
  69.2 5.3 conditional.19
  69.4 5.1 fusion.124
  76.4 8.7 %collective-permute-done.4 = bf16[128,1024]{1,0:T(8,128)(2,1)S(1)} collective-permute-done((bf16[128,1024]{1,0:T(8,128)(2,1)S(1)}, bf16[128,1024]{1,0:T(8,128)(2,1)S(1)}, u32[]{:S(2)}, u32[]{:S(2)}) %collective-permute-start.4) | collective-permute-done | bytes 262176 | tf_op jit(solution)/shard_map/ppermute | solution.py:12
  85.2 5.3 conditional.20
  85.4 5.1 fusion.155
  92.4 8.7 %collective-permute-done.5 = bf16[128,1024]{1,0:T(8,128)(2,1)S(1)} collective-permute-done((bf16[128,1024]{1,0:T(8,128)(2,1)S(1)}, bf16[128,1024]{1,0:T(8,128)(2,1)S(1)}, u32[]{:S(2)}, u32[]{:S(2)}) %collective-permute-start.5) | collective-permute-done | bytes 262176 | tf_op jit(solution)/shard_map/ppermute | solution.py:12
  101.2 5.5 conditional.21
  101.6 5.1 fusion.186
  108.6 9.1 %collective-permute-done.6 = bf16[128,1024]{1,0:T(8,128)(2,1)S(1)} collective-permute-done((bf16[128,1024]{1,0:T(8,128)(2,1)S(1)}, bf16[128,1024]{1,0:T(8,128)(2,1)S(1)}, u32[]{:S(2)}, u32[]{:S(2)}) %collective-permute-start.6) | collective-permute-done | bytes 262176 | tf_op jit(solution)/shard_map/ppermute | solution.py:12
  117.7 5.3 conditional.22
  117.9 5.1 fusion.217
  125.0 14.4 %collective-permute-done.7 = bf16[128,1024]{1,0:T(8,128)(2,1)S(1)} collective-permute-done((bf16[128,1024]{1,0:T(8,128)(2,1)S(1)}, bf16[128,1024]{1,0:T(8,128)(2,1)S(1)}, u32[]{:S(2)}, u32[]{:S(2)}) %collective-permute-start.7) | collective-permute-done | bytes 262176 | tf_op jit(solution)/shard_map/ppermute | solution.py:12
  139.4 5.3 conditional.23
  139.6 5.2 fusion.248
  146.7 11.1 %collective-permute-done.8 = bf16[128,1024]{1,0:T(8,128)(2,1)S(1)} collective-permute-done((bf16[128,1024]{1,0:T(8,128)(2,1)S(1)}, bf16[128,1024]{1,0:T(8,128)(2,1)S(1)}, u32[]{:S(2)}, u32[]{:S(2)}) %collective-permute-start.8) | collective-permute-done | bytes 262176 | tf_op jit(solution)/shard_map/ppermute | solution.py:12
  157.8 5.3 conditional.24
  158.0 5.1 fusion.279
  163.1 5.6 collective-permute-start.9
  168.7 8.2 %collective-permute-done.9 = bf16[128,1024]{1,0:T(8,128)(2,1)S(1)} collective-permute-done((bf16[128,1024]{1,0:T(8,128)(2,1)S(1)}, bf16[128,1024]{1,0:T(8,128)(2,1)S(1)}, u32[]{:S(2)}, u32[]{:S(2)}) %collective-permute-start.9) | collective-permute-done | bytes 262176 | tf_op jit(solution)/shard_map/ppermute | solution.py:12
  176.9 8.4 %collective-permute-start.10 = (bf16[128,1024]{1,0:T(8,128)(2,1)S(1)}, bf16[128,1024]{1,0:T(8,128)(2,1)S(1)}, u32[]{:S(2)}, u32[]{:S(2)}) collective-permute-start(bf16[128,1024]{1,0:T(8,128)(2,1)S(1)} %get-tuple-element.261), channel_id=1, source_target_pairs={{0,32},{32,64},{64,96},{96,128},{128,160},{160,192},{192,224},{1,3... | collective-permute-start | bytes 786440 | tf_op jit(solution)/shard_map/ppermute | solution.py:12
  185.4 3.9 collective-permute-done.10
  189.3 6.2 collective-permute-start.11
  195.6 6.6 collective-permute-done.11
  203.4 9.3 %collective-permute-start.12 = (bf16[128,1024]{1,0:T(8,128)(2,1)S(1)}, bf16[128,1024]{1,0:T(8,128)(2,1)S(1)}, u32[]{:S(2)}, u32[]{:S(2)}) collective-permute-start(bf16[128,1024]{1,0:T(8,128)(2,1)S(1)} %get-tuple-element.263), channel_id=1, source_target_pairs={{0,32},{32,64},{64,96},{96,128},{128,160},{160,192},{192,224},{1,3... | collective-permute-start | bytes 786440 | tf_op jit(solution)/shard_map/ppermute | solution.py:12
  212.8 3.8 collective-permute-done.12
  216.6 6.9 collective-permute-start.13
  223.6 3.8 collective-permute-done.13
  229.0 32.9 %all_gather.14 = bf16[256,1024]{1,0:T(8,128)(2,1)S(1)} all-gather(bf16[8,1024]{1,0:T(8,128)(2,1)S(1)} %copy-done.2), channel_id=1, replica_groups=mesh['segment'=8,'dp'=32] {'dp'}, dimensions={0}, use_global_device_ids=true | all-gather | bytes 540672 | tf_op jit(solution)/shard_map/all_gather | solution.py:96
  261.9 3.7 fusion.467
  265.7 2.7 fusion.484
  268.5 91.8 %all-reduce.2.cloned.1.call-done = bf16[1024,1024]{1,0:T(8,128)(2,1)} async-done(((bf16[1024,1024]{1,0:T(8,128)(2,1)}), bf16[1024,1024]{1,0:T(8,128)(2,1)}) %all-reduce.2.cloned.1.call-update) | async-done | bytes 2097168 | tf_op jit(solution)/shard_map/psum | solution.py:17
  361.4 92.7 %reduce-scatter.6.cloned.1.call-done = f32[128,1024]{1,0:T(8,128)} async-done(((f32[1024,1024]{1,0:T(8,128)}), f32[128,1024]{1,0:T(8,128)}) %reduce-scatter.6.cloned.1.call-update) | async-done | bytes 524304 | tf_op jit(solution)/shard_map/reduce_scatter | solution.py:101
  455.4 2.0 fusion.477
  457.5 59.0 %all-gather.7.cloned.1.call-done = bf16[1024,1024]{1,0:T(8,128)(2,1)} async-done(((bf16[128,1024]{1,0:T(8,128)(2,1)}), bf16[1024,1024]{1,0:T(8,128)(2,1)}) %all-gather.7.cloned.1.call-update) | async-done | bytes 2097168 | tf_op jit(solution)/shard_map/all_gather | solution.py:108
  516.5 3.4 fusion.483
  520.0 6.1 fusion.469
  528.0 107.9 %reduce-scatter.8.cloned.1.call-done = f32[8,1024]{1,0:T(8,128)} async-done(((f32[256,1024]{1,0:T(8,128)}), f32[8,1024]{1,0:T(8,128)}) %reduce-scatter.8.cloned.1.call-update) | async-done | bytes 32784 | tf_op jit(solution)/shard_map/reduce_scatter | solution.py:117
  635.9 117.7 %reduce-scatter.10.cloned.1.call-done = f32[64,256]{1,0:T(8,128)} async-done(((f32[2048,256]{1,0:T(8,128)}), f32[64,256]{1,0:T(8,128)}) %reduce-scatter.10.cloned.1.call-update) | async-done | bytes 65552
  (89 shorter events, 24.3 us)
Async XLA Ops:
  7.2 254.8 %all-gather.5.cloned.1.call-start = ((), (), s32[]{:S(2)}) async-start(), calls=%async_computation.3 | async-start | bytes 1081344 | tf_op jit(solution)/shard_map/all_gather | solution.py:95
  7.9 254.0 %all-gather.9.cloned.1.call-start = ((), (), s32[]{:S(2)}) async-start(), calls=%async_computation.8 | async-start | bytes 4718592 | tf_op jit(solution)/shard_map/all_gather | solution.py:98
  8.9 12.5 %copy-start = (bf16[1,1024,1024]{2,1,0:T(8,128)(2,1)S(1)}, bf16[1,1024,1024]{2,1,0:T(8,128)(2,1)}, u32[]{:S(2)}) copy-start(bf16[1,1024,1024]{2,1,0:T(8,128)(2,1)} %param.37) | copy-start | bytes 6291460
  9.0 12.5 %collective-permute-start = (bf16[128,1024]{1,0:T(8,128)(2,1)S(1)}, bf16[128,1024]{1,0:T(8,128)(2,1)S(1)}, u32[]{:S(2)}, u32[]{:S(2)}) collective-permute-start(bf16[128,1024]{1,0:T(8,128)(2,1)S(1)} %get-tuple-element.251), channel_id=1, source_target_pairs={{0,32},{32,64},{64,96},{96,128},{128,160},{160,192},{192,224},{1,3... | collective-permute-start | bytes 786440 | tf_op jit(solution)/shard_map/ppermute | solution.py:12
  14.2 346.1 %all-reduce.2.cloned.1.call-start = ((), (), s32[]{:S(2)}) async-start(), calls=%async_computation.5 | async-start | bytes 4194304 | tf_op jit(solution)/shard_map/psum | solution.py:17
  21.5 15.4 %collective-permute-start.1 = (bf16[128,1024]{1,0:T(8,128)(2,1)S(1)}, bf16[128,1024]{1,0:T(8,128)(2,1)S(1)}, u32[]{:S(2)}, u32[]{:S(2)}) collective-permute-start(bf16[128,1024]{1,0:T(8,128)(2,1)S(1)} %get-tuple-element.252), channel_id=1, source_target_pairs={{0,32},{32,64},{64,96},{96,128},{128,160},{160,192},{192,224},{1,3... | collective-permute-start | bytes 786440 | tf_op jit(solution)/shard_map/ppermute | solution.py:12
  42.3 10.8 %collective-permute-start.2 = (bf16[128,1024]{1,0:T(8,128)(2,1)S(1)}, bf16[128,1024]{1,0:T(8,128)(2,1)S(1)}, u32[]{:S(2)}, u32[]{:S(2)}) collective-permute-start(bf16[128,1024]{1,0:T(8,128)(2,1)S(1)} %get-tuple-element.253), channel_id=1, source_target_pairs={{0,32},{32,64},{64,96},{96,128},{128,160},{160,192},{192,224},{1,3... | collective-permute-start | bytes 786440 | tf_op jit(solution)/shard_map/ppermute | solution.py:12
  58.4 10.8 %collective-permute-start.3 = (bf16[128,1024]{1,0:T(8,128)(2,1)S(1)}, bf16[128,1024]{1,0:T(8,128)(2,1)S(1)}, u32[]{:S(2)}, u32[]{:S(2)}) collective-permute-start(bf16[128,1024]{1,0:T(8,128)(2,1)S(1)} %get-tuple-element.254), channel_id=1, source_target_pairs={{0,32},{32,64},{64,96},{96,128},{128,160},{160,192},{192,224},{1,3... | collective-permute-start | bytes 786440 | tf_op jit(solution)/shard_map/ppermute | solution.py:12
  74.5 10.7 %collective-permute-start.4 = (bf16[128,1024]{1,0:T(8,128)(2,1)S(1)}, bf16[128,1024]{1,0:T(8,128)(2,1)S(1)}, u32[]{:S(2)}, u32[]{:S(2)}) collective-permute-start(bf16[128,1024]{1,0:T(8,128)(2,1)S(1)} %get-tuple-element.255), channel_id=1, source_target_pairs={{0,32},{32,64},{64,96},{96,128},{128,160},{160,192},{192,224},{1,3... | collective-permute-start | bytes 786440 | tf_op jit(solution)/shard_map/ppermute | solution.py:12
  90.5 10.7 %collective-permute-start.5 = (bf16[128,1024]{1,0:T(8,128)(2,1)S(1)}, bf16[128,1024]{1,0:T(8,128)(2,1)S(1)}, u32[]{:S(2)}, u32[]{:S(2)}) collective-permute-start(bf16[128,1024]{1,0:T(8,128)(2,1)S(1)} %get-tuple-element.256), channel_id=1, source_target_pairs={{0,32},{32,64},{64,96},{96,128},{128,160},{160,192},{192,224},{1,3... | collective-permute-start | bytes 786440 | tf_op jit(solution)/shard_map/ppermute | solution.py:12
  106.7 11.0 %collective-permute-start.6 = (bf16[128,1024]{1,0:T(8,128)(2,1)S(1)}, bf16[128,1024]{1,0:T(8,128)(2,1)S(1)}, u32[]{:S(2)}, u32[]{:S(2)}) collective-permute-start(bf16[128,1024]{1,0:T(8,128)(2,1)S(1)} %get-tuple-element.257), channel_id=1, source_target_pairs={{0,32},{32,64},{64,96},{96,128},{128,160},{160,192},{192,224},{1,3... | collective-permute-start | bytes 786440 | tf_op jit(solution)/shard_map/ppermute | solution.py:12
  123.0 16.3 %collective-permute-start.7 = (bf16[128,1024]{1,0:T(8,128)(2,1)S(1)}, bf16[128,1024]{1,0:T(8,128)(2,1)S(1)}, u32[]{:S(2)}, u32[]{:S(2)}) collective-permute-start(bf16[128,1024]{1,0:T(8,128)(2,1)S(1)} %get-tuple-element.258), channel_id=1, source_target_pairs={{0,32},{32,64},{64,96},{96,128},{128,160},{160,192},{192,224},{1,3... | collective-permute-start | bytes 786440 | tf_op jit(solution)/shard_map/ppermute | solution.py:12
  144.7 13.0 %collective-permute-start.8 = (bf16[128,1024]{1,0:T(8,128)(2,1)S(1)}, bf16[128,1024]{1,0:T(8,128)(2,1)S(1)}, u32[]{:S(2)}, u32[]{:S(2)}) collective-permute-start(bf16[128,1024]{1,0:T(8,128)(2,1)S(1)} %get-tuple-element.259), channel_id=1, source_target_pairs={{0,32},{32,64},{64,96},{96,128},{128,160},{160,192},{192,224},{1,3... | collective-permute-start | bytes 786440 | tf_op jit(solution)/shard_map/ppermute | solution.py:12
  163.1 13.8 %collective-permute-start.9 = (bf16[128,1024]{1,0:T(8,128)(2,1)S(1)}, bf16[128,1024]{1,0:T(8,128)(2,1)S(1)}, u32[]{:S(2)}, u32[]{:S(2)}) collective-permute-start(bf16[128,1024]{1,0:T(8,128)(2,1)S(1)} %get-tuple-element.260), channel_id=1, source_target_pairs={{0,32},{32,64},{64,96},{96,128},{128,160},{160,192},{192,224},{1,3... | collective-permute-start | bytes 786440 | tf_op jit(solution)/shard_map/ppermute | solution.py:12
  176.9 12.3 %collective-permute-start.10 = (bf16[128,1024]{1,0:T(8,128)(2,1)S(1)}, bf16[128,1024]{1,0:T(8,128)(2,1)S(1)}, u32[]{:S(2)}, u32[]{:S(2)}) collective-permute-start(bf16[128,1024]{1,0:T(8,128)(2,1)S(1)} %get-tuple-element.261), channel_id=1, source_target_pairs={{0,32},{32,64},{64,96},{96,128},{128,160},{160,192},{192,224},{1,3... | collective-permute-start | bytes 786440 | tf_op jit(solution)/shard_map/ppermute | solution.py:12
  189.3 12.8 %collective-permute-start.11 = (bf16[128,1024]{1,0:T(8,128)(2,1)S(1)}, bf16[128,1024]{1,0:T(8,128)(2,1)}, u32[]{:S(2)}, u32[]{:S(2)}) collective-permute-start(bf16[128,1024]{1,0:T(8,128)(2,1)S(1)} %get-tuple-element.262), channel_id=1, source_target_pairs={{0,32},{32,64},{64,96},{96,128},{128,160},{160,192},{192,224},{1,3... | collective-permute-start | bytes 786440 | tf_op jit(solution)/shard_map/ppermute | solution.py:12
  203.4 13.2 %collective-permute-start.12 = (bf16[128,1024]{1,0:T(8,128)(2,1)S(1)}, bf16[128,1024]{1,0:T(8,128)(2,1)S(1)}, u32[]{:S(2)}, u32[]{:S(2)}) collective-permute-start(bf16[128,1024]{1,0:T(8,128)(2,1)S(1)} %get-tuple-element.263), channel_id=1, source_target_pairs={{0,32},{32,64},{64,96},{96,128},{128,160},{160,192},{192,224},{1,3... | collective-permute-start | bytes 786440 | tf_op jit(solution)/shard_map/ppermute | solution.py:12
  216.6 10.8 %collective-permute-start.13 = (bf16[128,1024]{1,0:T(8,128)(2,1)S(1)}, bf16[128,1024]{1,0:T(8,128)(2,1)S(1)}, u32[]{:S(2)}, u32[]{:S(2)}) collective-permute-start(bf16[128,1024]{1,0:T(8,128)(2,1)S(1)} %get-tuple-element.264), channel_id=1, source_target_pairs={{0,32},{32,64},{64,96},{96,128},{128,160},{160,192},{192,224},{1,3... | collective-permute-start | bytes 786440 | tf_op jit(solution)/shard_map/ppermute | solution.py:12
  227.4 1.6 copy-start.2
  229.0 225.1 %reduce-scatter.6.cloned.1.call-start = ((), (), s32[]{:S(2)}) async-start(), calls=%async_computation.4 | async-start | bytes 4718592 | tf_op jit(solution)/shard_map/reduce_scatter | solution.py:101
  265.7 250.9 %copy-start.3 = (f32[1024,256]{1,0:T(8,128)}, f32[1024,256]{1,0:T(8,128)S(1)}, u32[]{:S(2)}) copy-start(f32[1024,256]{1,0:T(8,128)S(1)} %fusion.467) | copy-start | bytes 3145732
  268.4 248.1 %all-gather.7.cloned.1.call-start = ((), (), s32[]{:S(2)}) async-start(), calls=%async_computation.6 | async-start | bytes 2359296 | tf_op jit(solution)/shard_map/all_gather | solution.py:108
  457.5 178.4 %reduce-scatter.8.cloned.1.call-start = ((), (), s32[]{:S(2)}) async-start(), calls=%async_computation.7 | async-start | bytes 1081344 | tf_op jit(solution)/shard_map/reduce_scatter | solution.py:117
  519.9 233.6 %reduce-scatter.10.cloned.1.call-start = ((), (), s32[]{:S(2)}) async-start(), calls=%async_computation.9 | async-start | bytes 2162688
Sparse Core Ops, SparseCore 0:
  9.8 66.5 all-gather.4
  79.1 94.0 all-gather.8
  229.1 131.1 all-reduce.1
  364.3 89.7 reduce-scatter.5
  457.6 58.9 all-gather.6
  520.1 115.7 reduce-scatter.7
  639.1 114.3 reduce-scatter.9
where the time goes:
time: 761 us; the launch traced here: 760 us
  waiting for transfers between devices  584 us (77%)
  starting transfers between devices  59.6 us (8%)
  matrix products  56.8 us (7%)
  blocking collectives  32.9 us (4%)
  between operations  14.6 us (2%)
  other arithmetic  9.31 us (1%)
    unnamed x8, waiting for transfers between devices  118 us
    ppermute x14, waiting for transfers between devices, shifted(): return lax.ppermute(block, axis, route)  114 us
    reduce_scatter x1, waiting for transfers between devices, on_device(): lax.psum_scatter(grad_second, 'dp', scatter_dimension=0, tiled=True)  108 us
    reduce_scatter x1, waiting for transfers between devices, on_device(): lax.psum_scatter(jnp.dot(activated, second_block, preferred_element_type=...  92.7 us
    psum x1, waiting for transfers between devices, from_root(): return lax.psum(block, axis)  91.8 us
    ppermute x14, starting transfers between devices, shifted(): return lax.ppermute(block, axis, route)  59.4 us
    all_gather x1, waiting for transfers between devices, on_device(): grad_all = lax.all_gather(grad_own, 'segment', axis=0, tiled=True)  59 us
    dot_general x8, matrix products, encoder_layer(): jnp.dot(inner, weight_out, preferred_element_type=jnp.float32)  40.9 us
  transfers between devices with their start and end apart: 21, of which 19 were waited for; matrix products, arithmetic and copies ran while one was open for 8% of the time, Pallas kernels for 0%

commit v1 on v0

--- a/solution.py
+++ b/solution.py
@@ -14,7 +14,7 @@
 
 def from_root(block, axis, holder):
     block = jnp.where(lax.axis_index(axis) == holder, block, jnp.zeros_like(block))
-    return lax.psum(block, axis)
+    return jnp.sum(lax.all_gather(block, axis), axis=0)
 
 
 def encoder_layer(hidden, scale_row, weight_in, weight_out):

time: 761 us -> 834 us (1.096)
  waiting for transfers between devices: 584 us -> 647 us
    all_gather x0 -> x1, waiting for transfers between devices: none -> 165 us  [from_root(): return jnp.sum(lax.all_gather(block, axis), axis=0)]
    psum x1 -> x0, waiting for transfers between devices: 91.8 us -> none  [from_root(): return lax.psum(block, axis)]
    reduce_scatter x1, waiting for transfers between devices: 92.7 us -> 83.2 us  [on_device(): lax.psum_scatter(jnp.dot(activated, second_block, preferred_element_type=...]
    reduce_sum x0 -> x1, other arithmetic: none -> 9.46 us  [from_root(): return jnp.sum(lax.all_gather(block, axis), axis=0)]
where the time goes in v1:
time: 834 us; the launch traced here: 833 us
  waiting for transfers between devices  647 us (78%)
  starting transfers between devices  60.6 us (7%)
  matrix products  57.1 us (7%)
  blocking collectives  33.7 us (4%)
  other arithmetic  16.8 us (2%)
  between operations  14.6 us (2%)
    all_gather x1, waiting for transfers between devices, from_root(): return jnp.sum(lax.all_gather(block, axis), axis=0)  165 us
    unnamed x8, waiting for transfers between devices  118 us
    ppermute x14, waiting for transfers between devices, shifted(): return lax.ppermute(block, axis, route)  114 us
    reduce_scatter x1, waiting for transfers between devices, on_device(): lax.psum_scatter(grad_second, 'dp', scatter_dimension=0, tiled=True)  108 us
    reduce_scatter x1, waiting for transfers between devices, on_device(): lax.psum_scatter(jnp.dot(activated, second_block, preferred_element_type=...  83.2 us
    ppermute x14, starting transfers between devices, shifted(): return lax.ppermute(block, axis, route)  60 us
    all_gather x1, waiting for transfers between devices, on_device(): grad_all = lax.all_gather(grad_own, 'segment', axis=0, tiled=True)  59 us
    dot_general x8, matrix products, encoder_layer(): jnp.dot(inner, weight_out, preferred_element_type=jnp.float32)  40.9 us
  transfers between devices with their start and end apart: 21, of which 19 were waited for; matrix products, arithmetic and copies ran while one was open for 8% of the time, Pallas kernels for 0%

profile of v1, /device:TPU:2, one launch (start us, length us, event | category | flops | bytes accessed | tf_op | source)
XLA Modules:
  0.0 833.3 jit_solution(4074723447263147708)
XLA Ops:
  9.0 5.2 collective-permute-start
  14.2 7.2 collective-permute-done
  21.5 4.2 collective-permute-start.1
  25.8 11.1 %collective-permute-done.1 = bf16[128,1024]{1,0:T(8,128)(2,1)S(1)} collective-permute-done((bf16[128,1024]{1,0:T(8,128)(2,1)S(1)}, bf16[128,1024]{1,0:T(8,128)(2,1)S(1)}, u32[]{:S(2)}, u32[]{:S(2)}) %collective-permute-start.1) | collective-permute-done | bytes 262176 | tf_op jit(solution)/shard_map/ppermute | solution.py:12
  36.9 5.3 conditional.17
  37.1 5.1 fusion.62
  44.2 8.8 %collective-permute-done.2 = bf16[128,1024]{1,0:T(8,128)(2,1)S(1)} collective-permute-done((bf16[128,1024]{1,0:T(8,128)(2,1)S(1)}, bf16[128,1024]{1,0:T(8,128)(2,1)S(1)}, u32[]{:S(2)}, u32[]{:S(2)}) %collective-permute-start.2) | collective-permute-done | bytes 262176 | tf_op jit(solution)/shard_map/ppermute | solution.py:12
  53.1 5.3 conditional.18
  53.3 5.1 fusion.93
  60.3 8.8 %collective-permute-done.3 = bf16[128,1024]{1,0:T(8,128)(2,1)S(1)} collective-permute-done((bf16[128,1024]{1,0:T(8,128)(2,1)S(1)}, bf16[128,1024]{1,0:T(8,128)(2,1)S(1)}, u32[]{:S(2)}, u32[]{:S(2)}) %collective-permute-start.3) | collective-permute-done | bytes 262176 | tf_op jit(solution)/shard_map/ppermute | solution.py:12
  69.2 5.3 conditional.19
  69.4 5.1 fusion.124
  76.4 8.7 %collective-permute-done.4 = bf16[128,1024]{1,0:T(8,128)(2,1)S(1)} collective-permute-done((bf16[128,1024]{1,0:T(8,128)(2,1)S(1)}, bf16[128,1024]{1,0:T(8,128)(2,1)S(1)}, u32[]{:S(2)}, u32[]{:S(2)}) %collective-permute-start.4) | collective-permute-done | bytes 262176 | tf_op jit(solution)/shard_map/ppermute | solution.py:12
  85.2 5.3 conditional.20
  85.4 5.1 fusion.155
  92.4 8.7 %collective-permute-done.5 = bf16[128,1024]{1,0:T(8,128)(2,1)S(1)} collective-permute-done((bf16[128,1024]{1,0:T(8,128)(2,1)S(1)}, bf16[128,1024]{1,0:T(8,128)(2,1)S(1)}, u32[]{:S(2)}, u32[]{:S(2)}) %collective-permute-start.5) | collective-permute-done | bytes 262176 | tf_op jit(solution)/shard_map/ppermute | solution.py:12
  101.2 5.5 conditional.21
  101.6 5.1 fusion.186
  108.6 9.1 %collective-permute-done.6 = bf16[128,1024]{1,0:T(8,128)(2,1)S(1)} collective-permute-done((bf16[128,1024]{1,0:T(8,128)(2,1)S(1)}, bf16[128,1024]{1,0:T(8,128)(2,1)S(1)}, u32[]{:S(2)}, u32[]{:S(2)}) %collective-permute-start.6) | collective-permute-done | bytes 262176 | tf_op jit(solution)/shard_map/ppermute | solution.py:12
  117.7 5.3 conditional.22
  117.9 5.1 fusion.217
  125.0 14.4 %collective-permute-done.7 = bf16[128,1024]{1,0:T(8,128)(2,1)S(1)} collective-permute-done((bf16[128,1024]{1,0:T(8,128)(2,1)S(1)}, bf16[128,1024]{1,0:T(8,128)(2,1)S(1)}, u32[]{:S(2)}, u32[]{:S(2)}) %collective-permute-start.7) | collective-permute-done | bytes 262176 | tf_op jit(solution)/shard_map/ppermute | solution.py:12
  139.4 5.3 conditional.23
  139.6 5.2 fusion.248
  146.7 11.1 %collective-permute-done.8 = bf16[128,1024]{1,0:T(8,128)(2,1)S(1)} collective-permute-done((bf16[128,1024]{1,0:T(8,128)(2,1)S(1)}, bf16[128,1024]{1,0:T(8,128)(2,1)S(1)}, u32[]{:S(2)}, u32[]{:S(2)}) %collective-permute-start.8) | collective-permute-done | bytes 262176 | tf_op jit(solution)/shard_map/ppermute | solution.py:12
  157.8 5.3 conditional.24
  158.0 5.1 fusion.279
  163.1 5.6 collective-permute-start.9
  168.7 8.2 collective-permute-done.9
  176.9 8.4 %collective-permute-start.10 = (bf16[128,1024]{1,0:T(8,128)(2,1)S(1)}, bf16[128,1024]{1,0:T(8,128)(2,1)S(1)}, u32[]{:S(2)}, u32[]{:S(2)}) collective-permute-start(bf16[128,1024]{1,0:T(8,128)(2,1)S(1)} %get-tuple-element.316), channel_id=1, source_target_pairs={{0,32},{32,64},{64,96},{96,128},{128,160},{160,192},{192,224},{1,3... | collective-permute-start | bytes 786440 | tf_op jit(solution)/shard_map/ppermute | solution.py:12
  185.4 3.8 collective-permute-done.10
  189.3 6.2 collective-permute-start.11
  195.6 5.7 collective-permute-done.11
  201.6 10.1 %collective-permute-start.12 = (bf16[128,1024]{1,0:T(8,128)(2,1)S(1)}, bf16[128,1024]{1,0:T(8,128)(2,1)S(1)}, u32[]{:S(2)}, u32[]{:S(2)}) collective-permute-start(bf16[128,1024]{1,0:T(8,128)(2,1)S(1)} %get-tuple-element.318), channel_id=1, source_target_pairs={{0,32},{32,64},{64,96},{96,128},{128,160},{160,192},{192,224},{1,3... | collective-permute-start | bytes 786440 | tf_op jit(solution)/shard_map/ppermute | solution.py:12
  211.8 3.8 collective-permute-done.12
  215.7 6.8 collective-permute-start.13
  222.5 3.8 collective-permute-done.13
  228.0 33.7 %all_gather.18 = bf16[256,1024]{1,0:T(8,128)(2,1)S(1)} all-gather(bf16[8,1024]{1,0:T(8,128)(2,1)S(1)} %copy-done.1), channel_id=1, replica_groups=mesh['segment'=8,'dp'=32] {'dp'}, dimensions={0}, use_global_device_ids=true | all-gather | bytes 540672 | tf_op jit(solution)/shard_map/all_gather | solution.py:96
  261.8 3.7 fusion.468
  266.5 2.7 fusion.485
  269.3 164.8 %all-gather.8.cloned.1.call-done = bf16[8,1024,1024]{2,1,0:T(8,128)(2,1)} async-done(((bf16[1,1024,1024]{2,1,0:T(8,128)(2,1)}), bf16[8,1024,1024]{2,1,0:T(8,128)(2,1)}) %all-gather.8.cloned.1.call-update) | async-done | bytes 16777232 | tf_op jit(solution)/shard_map/all_gather | solution.py:17
  434.0 9.5 %reduce_sum.174 = bf16[1024,1024]{1,0:T(8,128)(2,1)S(1)} reduce(bf16[8,1024,1024]{2,1,0:T(8,128)(2,1)} %all-gather.8.cloned.1.call-done, bf16[]{:T(256)} %constant.266.clone.1), dimensions={0}, to_apply=%region_46.47 | reduce | flops 7340032 | bytes 18874370 | tf_op jit(solution)/shard_map/reduce_sum | solution.py:17
  443.6 83.2 %reduce-scatter.6.cloned.1.call-done = f32[128,1024]{1,0:T(8,128)} async-done(((f32[1024,1024]{1,0:T(8,128)}), f32[128,1024]{1,0:T(8,128)}) %reduce-scatter.6.cloned.1.call-update) | async-done | bytes 524304 | tf_op jit(solution)/shard_map/reduce_scatter | solution.py:101
  530.1 59.0 %all-gather.10.cloned.1.call-done = bf16[1024,1024]{1,0:T(8,128)(2,1)} async-done(((bf16[128,1024]{1,0:T(8,128)(2,1)}), bf16[1024,1024]{1,0:T(8,128)(2,1)}) %all-gather.10.cloned.1.call-update) | async-done | bytes 2097168 | tf_op jit(solution)/shard_map/all_gather | solution.py:108
  589.1 3.7 fusion.484
  593.1 6.1 fusion.470
  601.1 107.7 %reduce-scatter.8.cloned.1.call-done = f32[8,1024]{1,0:T(8,128)} async-done(((f32[256,1024]{1,0:T(8,128)}), f32[8,1024]{1,0:T(8,128)}) %reduce-scatter.8.cloned.1.call-update) | async-done | bytes 32784 | tf_op jit(solution)/shard_map/reduce_scatter | solution.py:117
  708.8 117.7 %reduce-scatter.10.cloned.1.call-done = f32[64,256]{1,0:T(8,128)} async-done(((f32[2048,256]{1,0:T(8,128)}), f32[64,256]{1,0:T(8,128)}) %reduce-scatter.10.cloned.1.call-update) | async-done | bytes 65552
  (91 shorter events, 25.5 us)
Async XLA Ops:
  7.2 254.6 %all-gather.6.cloned.1.call-start = ((), (), s32[]{:S(2)}) async-start(), calls=%async_computation.3 | async-start | bytes 1081344 | tf_op jit(solution)/shard_map/all_gather | solution.py:95
  7.9 253.9 %all-gather.12.cloned.1.call-start = ((), (), s32[]{:S(2)}) async-start(), calls=%async_computation.8 | async-start | bytes 4718592 | tf_op jit(solution)/shard_map/all_gather | solution.py:98
  8.9 12.5 %copy-start = (bf16[1,1024,1024]{2,1,0:T(8,128)(2,1)S(1)}, bf16[1,1024,1024]{2,1,0:T(8,128)(2,1)}, u32[]{:S(2)}) copy-start(bf16[1,1024,1024]{2,1,0:T(8,128)(2,1)} %param.37) | copy-start | bytes 6291460
  9.0 12.5 %collective-permute-start = (bf16[128,1024]{1,0:T(8,128)(2,1)S(1)}, bf16[128,1024]{1,0:T(8,128)(2,1)S(1)}, u32[]{:S(2)}, u32[]{:S(2)}) collective-permute-start(bf16[128,1024]{1,0:T(8,128)(2,1)S(1)} %get-tuple-element.306), channel_id=1, source_target_pairs={{0,32},{32,64},{64,96},{96,128},{128,160},{160,192},{192,224},{1,3... | collective-permute-start | bytes 786440 | tf_op jit(solution)/shard_map/ppermute | solution.py:12
  21.5 15.4 %collective-permute-start.1 = (bf16[128,1024]{1,0:T(8,128)(2,1)S(1)}, bf16[128,1024]{1,0:T(8,128)(2,1)S(1)}, u32[]{:S(2)}, u32[]{:S(2)}) collective-permute-start(bf16[128,1024]{1,0:T(8,128)(2,1)S(1)} %get-tuple-element.307), channel_id=1, source_target_pairs={{0,32},{32,64},{64,96},{96,128},{128,160},{160,192},{192,224},{1,3... | collective-permute-start | bytes 786440 | tf_op jit(solution)/shard_map/ppermute | solution.py:12
  25.7 408.3 %all-gather.8.cloned.1.call-start = ((), (), s32[]{:S(2)}) async-start(), calls=%async_computation.5 | async-start | bytes 18874368 | tf_op jit(solution)/shard_map/all_gather | solution.py:17
  42.3 10.8 %collective-permute-start.2 = (bf16[128,1024]{1,0:T(8,128)(2,1)S(1)}, bf16[128,1024]{1,0:T(8,128)(2,1)S(1)}, u32[]{:S(2)}, u32[]{:S(2)}) collective-permute-start(bf16[128,1024]{1,0:T(8,128)(2,1)S(1)} %get-tuple-element.308), channel_id=1, source_target_pairs={{0,32},{32,64},{64,96},{96,128},{128,160},{160,192},{192,224},{1,3... | collective-permute-start | bytes 786440 | tf_op jit(solution)/shard_map/ppermute | solution.py:12
  58.4 10.8 %collective-permute-start.3 = (bf16[128,1024]{1,0:T(8,128)(2,1)S(1)}, bf16[128,1024]{1,0:T(8,128)(2,1)S(1)}, u32[]{:S(2)}, u32[]{:S(2)}) collective-permute-start(bf16[128,1024]{1,0:T(8,128)(2,1)S(1)} %get-tuple-element.309), channel_id=1, source_target_pairs={{0,32},{32,64},{64,96},{96,128},{128,160},{160,192},{192,224},{1,3... | collective-permute-start | bytes 786440 | tf_op jit(solution)/shard_map/ppermute | solution.py:12
  74.5 10.7 %collective-permute-start.4 = (bf16[128,1024]{1,0:T(8,128)(2,1)S(1)}, bf16[128,1024]{1,0:T(8,128)(2,1)S(1)}, u32[]{:S(2)}, u32[]{:S(2)}) collective-permute-start(bf16[128,1024]{1,0:T(8,128)(2,1)S(1)} %get-tuple-element.310), channel_id=1, source_target_pairs={{0,32},{32,64},{64,96},{96,128},{128,160},{160,192},{192,224},{1,3... | collective-permute-start | bytes 786440 | tf_op jit(solution)/shard_map/ppermute | solution.py:12
  90.5 10.7 %collective-permute-start.5 = (bf16[128,1024]{1,0:T(8,128)(2,1)S(1)}, bf16[128,1024]{1,0:T(8,128)(2,1)S(1)}, u32[]{:S(2)}, u32[]{:S(2)}) collective-permute-start(bf16[128,1024]{1,0:T(8,128)(2,1)S(1)} %get-tuple-element.311), channel_id=1, source_target_pairs={{0,32},{32,64},{64,96},{96,128},{128,160},{160,192},{192,224},{1,3... | collective-permute-start | bytes 786440 | tf_op jit(solution)/shard_map/ppermute | solution.py:12
  106.7 11.0 %collective-permute-start.6 = (bf16[128,1024]{1,0:T(8,128)(2,1)S(1)}, bf16[128,1024]{1,0:T(8,128)(2,1)S(1)}, u32[]{:S(2)}, u32[]{:S(2)}) collective-permute-start(bf16[128,1024]{1,0:T(8,128)(2,1)S(1)} %get-tuple-element.312), channel_id=1, source_target_pairs={{0,32},{32,64},{64,96},{96,128},{128,160},{160,192},{192,224},{1,3... | collective-permute-start | bytes 786440 | tf_op jit(solution)/shard_map/ppermute | solution.py:12
  123.0 16.3 %collective-permute-start.7 = (bf16[128,1024]{1,0:T(8,128)(2,1)S(1)}, bf16[128,1024]{1,0:T(8,128)(2,1)S(1)}, u32[]{:S(2)}, u32[]{:S(2)}) collective-permute-start(bf16[128,1024]{1,0:T(8,128)(2,1)S(1)} %get-tuple-element.313), channel_id=1, source_target_pairs={{0,32},{32,64},{64,96},{96,128},{128,160},{160,192},{192,224},{1,3... | collective-permute-start | bytes 786440 | tf_op jit(solution)/shard_map/ppermute | solution.py:12
  144.7 13.0 %collective-permute-start.8 = (bf16[128,1024]{1,0:T(8,128)(2,1)S(1)}, bf16[128,1024]{1,0:T(8,128)(2,1)S(1)}, u32[]{:S(2)}, u32[]{:S(2)}) collective-permute-start(bf16[128,1024]{1,0:T(8,128)(2,1)S(1)} %get-tuple-element.314), channel_id=1, source_target_pairs={{0,32},{32,64},{64,96},{96,128},{128,160},{160,192},{192,224},{1,3... | collective-permute-start | bytes 786440 | tf_op jit(solution)/shard_map/ppermute | solution.py:12
  163.1 13.8 %collective-permute-start.9 = (bf16[128,1024]{1,0:T(8,128)(2,1)S(1)}, bf16[128,1024]{1,0:T(8,128)(2,1)S(1)}, u32[]{:S(2)}, u32[]{:S(2)}) collective-permute-start(bf16[128,1024]{1,0:T(8,128)(2,1)S(1)} %get-tuple-element.315), channel_id=1, source_target_pairs={{0,32},{32,64},{64,96},{96,128},{128,160},{160,192},{192,224},{1,3... | collective-permute-start | bytes 786440 | tf_op jit(solution)/shard_map/ppermute | solution.py:12
  176.9 12.3 %collective-permute-start.10 = (bf16[128,1024]{1,0:T(8,128)(2,1)S(1)}, bf16[128,1024]{1,0:T(8,128)(2,1)S(1)}, u32[]{:S(2)}, u32[]{:S(2)}) collective-permute-start(bf16[128,1024]{1,0:T(8,128)(2,1)S(1)} %get-tuple-element.316), channel_id=1, source_target_pairs={{0,32},{32,64},{64,96},{96,128},{128,160},{160,192},{192,224},{1,3... | collective-permute-start | bytes 786440 | tf_op jit(solution)/shard_map/ppermute | solution.py:12
  189.3 12.0 %collective-permute-start.11 = (bf16[128,1024]{1,0:T(8,128)(2,1)S(1)}, bf16[128,1024]{1,0:T(8,128)(2,1)S(1)}, u32[]{:S(2)}, u32[]{:S(2)}) collective-permute-start(bf16[128,1024]{1,0:T(8,128)(2,1)S(1)} %get-tuple-element.317), channel_id=1, source_target_pairs={{0,32},{32,64},{64,96},{96,128},{128,160},{160,192},{192,224},{1,3... | collective-permute-start | bytes 786440 | tf_op jit(solution)/shard_map/ppermute | solution.py:12
  201.6 14.0 %collective-permute-start.12 = (bf16[128,1024]{1,0:T(8,128)(2,1)S(1)}, bf16[128,1024]{1,0:T(8,128)(2,1)S(1)}, u32[]{:S(2)}, u32[]{:S(2)}) collective-permute-start(bf16[128,1024]{1,0:T(8,128)(2,1)S(1)} %get-tuple-element.318), channel_id=1, source_target_pairs={{0,32},{32,64},{64,96},{96,128},{128,160},{160,192},{192,224},{1,3... | collective-permute-start | bytes 786440 | tf_op jit(solution)/shard_map/ppermute | solution.py:12
  215.7 10.7 %collective-permute-start.13 = (bf16[128,1024]{1,0:T(8,128)(2,1)S(1)}, bf16[128,1024]{1,0:T(8,128)(2,1)S(1)}, u32[]{:S(2)}, u32[]{:S(2)}) collective-permute-start(bf16[128,1024]{1,0:T(8,128)(2,1)S(1)} %get-tuple-element.319), channel_id=1, source_target_pairs={{0,32},{32,64},{64,96},{96,128},{128,160},{160,192},{192,224},{1,3... | collective-permute-start | bytes 786440 | tf_op jit(solution)/shard_map/ppermute | solution.py:12
  226.4 1.6 copy-start.1
  227.9 298.9 %reduce-scatter.6.cloned.1.call-start = ((), (), s32[]{:S(2)}) async-start(), calls=%async_computation.4 | async-start | bytes 4718592 | tf_op jit(solution)/shard_map/reduce_scatter | solution.py:101
  265.5 1.0 copy-start.2
  269.2 319.9 %all-gather.10.cloned.1.call-start = ((), (), s32[]{:S(2)}) async-start(), calls=%async_computation.6 | async-start | bytes 2359296 | tf_op jit(solution)/shard_map/all_gather | solution.py:108
  530.0 178.7 %reduce-scatter.8.cloned.1.call-start = ((), (), s32[]{:S(2)}) async-start(), calls=%async_computation.7 | async-start | bytes 1081344 | tf_op jit(solution)/shard_map/reduce_scatter | solution.py:117
  592.8 233.6 %reduce-scatter.10.cloned.1.call-start = ((), (), s32[]{:S(2)}) async-start(), calls=%async_computation.9 | async-start | bytes 2162688
Sparse Core Ops, SparseCore 0:
  9.8 66.5 all-gather.5
  79.1 94.0 all-gather.11
  228.1 205.9 all-gather.7
  438.0 88.7 reduce-scatter.5
  530.2 58.9 all-gather.9
  593.0 115.7 reduce-scatter.7
  712.0 114.3 reduce-scatter.9
